TPU v7x, 32 devices: a whole 2x2x4 slice. The times are simulated.
32 devices in a mesh: ta: 4 (over y, x), gz: 4 (over z), xy: 2 (over core).
Axes of the slice: x: 2, y: 2, z: 4, core: 2. Of those that a mesh axis runs over, the one named last changes fastest.
Arguments:
- links: float32 [4, 2, 3, 3, 8, 8, 256], P(None, None, None, None, 'ta', 'gz', 'xy'), may hold values from -1 to 1, as said below
- solutions: float32 [2, 2, 4, 3, 8, 8, 256], P(None, None, None, None, 'ta', 'gz', 'xy'), may hold values from -6 to 6
Outputs:
- force: float32 [4, 2, 3, 3, 8, 8, 256], P(None, None, None, None, 'ta', 'gz', 'xy')
Inputs may be any that keep to these rules, and one draw needn't show every extreme that they name: Each links[mu] at a site, read as a complex 3 x 3 matrix, is special unitary.
All inputs are finite; a program needn't handle non-finite values.
Results may differ from a plain program's by a relative error of at most 0.0001.
Values sent between devices are 32-bit elements; how exact they have to be, the bound alone decides.
A program may use at most 64 MiB of HBM per device.

v0:
```python
from functools import reduce

import jax
import jax.numpy as jnp
import numpy as np
from jax import lax
from jax.sharding import PartitionSpec as P

Y_LEN = 64


HOPPING = 0.125
PLAQUETTE = 0.5


def padded_2(x, sides, width):
    for axis, dim in sides:
        size, length = (lax.axis_size(axis), x.shape[dim])
        up = [(i, (i + 1) % size) for i in range(size)]
        down = [(j, i) for i, j in up]
        last = lax.slice_in_dim(x, length - width, length, axis=dim)
        initial = lax.slice_in_dim(x, 0, width, axis=dim)
        before = lax.ppermute(last, axis, up)
        after = lax.ppermute(initial, axis, down)
        x = jnp.concatenate([before, x, after], axis=dim)
    return x


def shifted(x, axis, by):
    length = lax.axis_size(axis)
    return lax.ppermute(x, axis, [(i, (i + by) % length) for i in range(length)])


def projectors():
    identity = np.eye(4)
    zeros = np.zeros((4, 4))
    gamma_time = (np.array([[0, 0, 1, 0], [0, 0, 0, 1], [1, 0, 0, 0], [0, 1, 0, 0]]), zeros)
    gamma_depth = (zeros, np.array([[0, 0, 1, 0], [0, 0, 0, -1], [-1, 0, 0, 0], [0, 1, 0, 0]]))
    gamma_across = (zeros, np.array([[0, 0, 0, 1], [0, 0, 1, 0], [0, -1, 0, 0], [-1, 0, 0, 0]]))
    gamma_along = (np.array([[0, 0, 0, -1], [0, 0, 1, 0], [0, 1, 0, 0], [-1, 0, 0, 0]]), zeros)
    result = []
    for gamma_pair in (gamma_time, gamma_depth, gamma_across, gamma_along):
        result.append(
            ((identity - gamma_pair[0], -gamma_pair[1]), (identity + gamma_pair[0], gamma_pair[1]))
        )
    return result


def shift_rows(source, stride, row_length):
    positions = lax.iota(jnp.int32, source.shape[-1]) % row_length
    if stride > 0:
        return jnp.where(
            positions == row_length - 1,
            jnp.roll(source, row_length - 1, -1),
            jnp.roll(source, -1, -1),
        )
    return jnp.where(positions == 0, jnp.roll(source, 1 - row_length, -1), jnp.roll(source, 1, -1))


def offset(direction, stride):
    if direction == 3:
        return ((0, 0, 0), stride)
    anchor = [0, 0, 0]
    anchor[direction] = stride
    return (tuple(anchor), 0)


def combine(first_anchor, second_anchor):
    return (
        first_anchor[0] + second_anchor[0],
        first_anchor[1] + second_anchor[1],
        first_anchor[2] + second_anchor[2],
    )


def window(padded, margin, anchor, extent, stride):
    time_start = margin + anchor[0]
    depth_start = margin + anchor[1]
    row_start = (margin + anchor[2]) * Y_LEN
    region = padded[
        ...,
        time_start : time_start + extent[0],
        depth_start : depth_start + extent[1],
        row_start : row_start + extent[2] * Y_LEN,
    ]
    if stride != 0:
        region = shift_rows(region, stride, Y_LEN)
    return region


def face_window(face_box, direction, stride, flat_shape):
    starts = [1, 1, 1]
    if direction < 3:
        starts[direction] = 1 + stride
    time_count = face_box.shape[4] - 2
    depth_count = face_box.shape[5] - 2
    row_number = face_box.shape[6] - 2
    region = face_box[
        ...,
        starts[0] : starts[0] + time_count,
        starts[1] : starts[1] + depth_count,
        starts[2] : starts[2] + row_number,
        :,
    ]
    if direction == 3:
        region = jnp.roll(region, -stride, -1)
    return region.reshape(flat_shape)


def matrix_product(left, right):
    left_real, left_imaginary = (left[0], left[1])
    right_real, right_imaginary = (right[0], right[1])
    real_part = jnp.sum(
        left_real[:, :, None] * right_real[None]
        - left_imaginary[:, :, None] * right_imaginary[None],
        axis=1,
    )
    imaginary_part = jnp.sum(
        left_real[:, :, None] * right_imaginary[None]
        + left_imaginary[:, :, None] * right_real[None],
        axis=1,
    )
    return jnp.stack([real_part, imaginary_part])


def dagger(matrix):
    return jnp.stack([jnp.swapaxes(matrix[0], 0, 1), -jnp.swapaxes(matrix[1], 0, 1)])


def colour_apply(matrix, spinor):
    matrix_real = matrix[0][None, None]
    matrix_imaginary = matrix[1][None, None]
    spinor_real = spinor[:, 0][:, :, None]
    spinor_imaginary = spinor[:, 1][:, :, None]
    real_part = jnp.sum(matrix_real * spinor_real - matrix_imaginary * spinor_imaginary, axis=3)
    imaginary_part = jnp.sum(
        matrix_real * spinor_imaginary + matrix_imaginary * spinor_real, axis=3
    )
    return jnp.stack([real_part, imaginary_part], axis=1)


def spin_apply(projector, spinor):
    spinor_real = spinor[:, 0]
    spinor_imaginary = spinor[:, 1]
    rows_real = []
    rows_imaginary = []
    for spin_row in range(4):
        terms_real = []
        terms_imaginary = []
        for spin_column in range(4):
            weight_real = float(projector[0][spin_row, spin_column])
            weight_imaginary = float(projector[1][spin_row, spin_column])
            terms_real.append(
                weight_real * spinor_real[:, spin_column]
                - weight_imaginary * spinor_imaginary[:, spin_column]
            )
            terms_imaginary.append(
                weight_real * spinor_imaginary[:, spin_column]
                + weight_imaginary * spinor_real[:, spin_column]
            )
        rows_real.append(reduce(jnp.add, terms_real))
        rows_imaginary.append(reduce(jnp.add, terms_imaginary))
    return jnp.stack([jnp.stack(rows_real, 1), jnp.stack(rows_imaginary, 1)], 1)


def spin_outer(upper_spinor, lower_spinor):
    upper_real = upper_spinor[:, 0][:, :, :, None]
    upper_imaginary = upper_spinor[:, 1][:, :, :, None]
    lower_real = lower_spinor[:, 0][:, :, None]
    lower_imaginary = lower_spinor[:, 1][:, :, None]
    real_part = jnp.sum(upper_real * lower_real + upper_imaginary * lower_imaginary, axis=(0, 1))
    imaginary_part = jnp.sum(
        upper_imaginary * lower_real - upper_real * lower_imaginary, axis=(0, 1)
    )
    return jnp.stack([real_part, imaginary_part])


def traceless_part(matrix):
    real_part = 0.5 * (matrix[0] - jnp.swapaxes(matrix[0], 0, 1))
    imaginary_part = 0.5 * (matrix[1] + jnp.swapaxes(matrix[1], 0, 1))
    trace_third = (imaginary_part[0, 0] + imaginary_part[1, 1] + imaginary_part[2, 2]) / 3.0
    identity = jnp.eye(3, dtype=matrix.dtype).reshape((3, 3) + (1,) * (matrix.ndim - 3))
    imaginary_part = imaginary_part - identity * trace_third
    return jnp.stack([real_part, imaginary_part])


def on_device(links, solutions):
    time_block = links.shape[4]
    depth_block = links.shape[5]
    row_count = links.shape[6] // Y_LEN
    link_box = padded_2(links, (("xy", 6),), Y_LEN)
    link_box = padded_2(link_box, (("ta", 4), ("gz", 5)), 1)
    time_rank = lax.axis_index("ta")
    time_ranks = lax.axis_size("ta")
    projector_list = projectors()
    zero_anchor = (0, 0, 0)
    force_extent = (time_block, depth_block, row_count)
    flat_shape = solutions.shape
    grid_shape = solutions.shape[:4] + (time_block, depth_block, row_count, Y_LEN)
    grid = solutions.reshape(grid_shape)
    face_box = padded_2(grid, (("ta", 4), ("gz", 5), ("xy", 6)), 1)
    positions = lax.iota(jnp.int32, time_block + 2)
    flipped = (positions == 0) & (time_rank == 0) | (positions == time_block + 1) & (
        time_rank == time_ranks - 1
    )
    factor = jnp.where(flipped, -1.0, 1.0).astype(face_box.dtype)
    face_box = face_box * factor[:, None, None, None]
    hop_terms = []
    for direction in range(4):
        minus_projector, plus_projector = projector_list[direction]
        behind_anchor, behind_stride = offset(direction, -1)
        link_here = window(link_box[direction], 1, zero_anchor, force_extent, 0)
        forward = colour_apply(
            link_here, spin_apply(minus_projector, face_window(face_box, direction, 1, flat_shape))
        )
        link_behind = window(link_box[direction], 1, behind_anchor, force_extent, behind_stride)
        backward = colour_apply(
            dagger(link_behind),
            spin_apply(plus_projector, face_window(face_box, direction, -1, flat_shape)),
        )
        hop_terms.append(forward + backward)
    partner_here = solutions - HOPPING * reduce(jnp.add, hop_terms)
    partner_grid = partner_here.reshape(grid_shape)
    time_face = shifted(partner_grid[..., 0:1, :, :, :], "ta", -1)
    time_face = time_face * jnp.where(time_rank == time_ranks - 1, -1.0, 1.0).astype(
        time_face.dtype
    )
    depth_face = shifted(partner_grid[..., :, 0:1, :, :], "gz", -1)
    row_face = shifted(partner_grid[..., :, :, 0:1, :], "xy", -1)
    ahead_partner = [
        jnp.concatenate([partner_grid[..., 1:, :, :, :], time_face], axis=4).reshape(flat_shape),
        jnp.concatenate([partner_grid[..., :, 1:, :, :], depth_face], axis=5).reshape(flat_shape),
        jnp.concatenate([partner_grid[..., :, :, 1:, :], row_face], axis=6).reshape(flat_shape),
        jnp.roll(partner_grid, -1, -1).reshape(flat_shape),
    ]
    ahead_solution = [face_window(face_box, direction, 1, flat_shape) for direction in range(4)]
    forces = []
    for direction in range(4):
        minus_projector, plus_projector = projector_list[direction]
        ahead_anchor, ahead_stride = offset(direction, 1)
        link_main = window(link_box[direction], 1, zero_anchor, force_extent, 0)
        pieces = []
        for second in range(4):
            if second == direction:
                continue
            side_anchor, side_stride = offset(second, 1)
            back_anchor, back_stride = offset(second, -1)
            link_second = window(link_box[second], 1, zero_anchor, force_extent, 0)
            upper_staple = matrix_product(
                matrix_product(
                    window(link_box[second], 1, ahead_anchor, force_extent, ahead_stride),
                    dagger(window(link_box[direction], 1, side_anchor, force_extent, side_stride)),
                ),
                dagger(link_second),
            )
            shifted_back = window(link_box[second], 1, back_anchor, force_extent, back_stride)
            corner_link = window(
                link_box[second],
                1,
                combine(ahead_anchor, back_anchor),
                force_extent,
                ahead_stride + back_stride,
            )
            lower_staple = matrix_product(
                matrix_product(
                    dagger(corner_link),
                    dagger(window(link_box[direction], 1, back_anchor, force_extent, back_stride)),
                ),
                shifted_back,
            )
            pieces.append(upper_staple + lower_staple)
        staple = reduce(jnp.add, pieces)
        fermion = spin_outer(
            spin_apply(minus_projector, ahead_solution[direction]), partner_here
        ) + spin_outer(spin_apply(plus_projector, ahead_partner[direction]), solutions)
        forces.append(
            traceless_part(matrix_product(link_main, PLAQUETTE * staple + HOPPING * fermion))
        )
    return jnp.stack(forces)


def solution(mesh):
    return jax.shard_map(
        on_device,
        mesh=mesh,
        in_specs=(
            P(None, None, None, None, "ta", "gz", "xy"),
            P(None, None, None, None, "ta", "gz", "xy"),
        ),
        out_specs=P(None, None, None, None, "ta", "gz", "xy"),
        check_vma=False,
    )
```

profile of v0, /device:TPU:0, one launch (start us, length us, event | category | flops | bytes accessed | tf_op | source)
XLA Modules:
  0.0 93.2 jit_solution(13900752231559104126)
XLA Ops:
  0.0 1.0 %copy.458 = f32[4,2,3,3,2,2,128]{6,4,5,3,2,1,0:T(2,128)S(1)} copy(f32[4,2,3,3,2,2,128]{6,5,4,3,2,1,0:T(2,128)} %param.2) | data formatting | bytes 294912 | tf_op args[0]
  1.9 1.1 %reshape.304 = f32[2,2,4,3,2,2,2,64]{7,6,5,4,3,2,1,0:T(2,128)S(1)} reshape(f32[2,2,4,3,2,2,128]{6,5,4,3,2,1,0:T(2,128)} %param.3) | data formatting | bytes 196608 | tf_op jit(solution)/shard_map/reshape | solution.py:200
  3.0 3.0 %collective-permute-start.6 = (f32[2,2,4,3,1,2,2,64]{7,6,5,4,3,2,0,1:T(2,128)S(1)}, f32[2,2,4,3,1,2,2,64]{7,6,5,4,3,2,0,1:T(2,128)S(1)}, u32[]{:S(2)}, u32[]{:S(2)}) collective-permute-start(f32[2,2,4,3,1,2,2,64]{7,6,5,4,3,2,0,1:T(2,128)S(1)} %copy.683), channel_id=1, source_target_pairs={{0,8},{8,16},{16,24},{24,0},{1,9},{9,17},{17,25},{25,1},{2,10},{10... | collective-permute-start | bytes 147464 | tf_op jit(solution)/shard_map/ppermute | solution.py:23
  6.0 1.0 %collective-permute-start.7 = (f32[2,2,4,3,1,2,2,64]{7,6,5,4,3,2,0,1:T(2,128)S(1)}, f32[2,2,4,3,1,2,2,64]{7,6,5,4,3,2,0,1:T(2,128)S(1)}, u32[]{:S(2)}, u32[]{:S(2)}) collective-permute-start(f32[2,2,4,3,1,2,2,64]{7,6,5,4,3,2,0,1:T(2,128)S(1)} %copy.684), channel_id=1, source_target_pairs={{8,0},{16,8},{24,16},{0,24},{9,1},{17,9},{25,17},{1,25},{10,2},{18... | collective-permute-start | bytes 147464 | tf_op jit(solution)/shard_map/ppermute | solution.py:24
  10.6 1.7 %collective-permute-done.7 = f32[2,2,4,3,1,2,2,64]{7,6,5,4,3,2,0,1:T(2,128)S(1)} collective-permute-done((f32[2,2,4,3,1,2,2,64]{7,6,5,4,3,2,0,1:T(2,128)S(1)}, f32[2,2,4,3,1,2,2,64]{7,6,5,4,3,2,0,1:T(2,128)S(1)}, u32[]{:S(2)}, u32[]{:S(2)}) %collective-permute-start.7) | collective-permute-done | bytes 49184 | tf_op jit(solution)/shard_map/ppermute | solution.py:24
  12.5 3.7 %collective-permute-start.9 = (f32[2,2,4,3,4,1,2,64]{7,6,5,4,3,2,0,1:T(2,128)S(1)}, f32[2,2,4,3,4,1,2,64]{7,6,5,4,3,2,0,1:T(2,128)S(1)}, u32[]{:S(2)}, u32[]{:S(2)}) collective-permute-start(f32[2,2,4,3,4,1,2,64]{7,6,5,4,3,2,0,1:T(2,128)S(1)} %get-tuple-element.204), channel_id=1, source_target_pairs={{2,0},{4,2},{6,4},{0,6},{3,1},{5,3},{7,5},{1,7},{10,8},{12,10},{14... | collective-permute-start | bytes 294920 | tf_op jit(solution)/shard_map/ppermute | solution.py:24
  17.0 1.5 %collective-permute-start.3 = (f32[4,2,3,3,1,2,256]{6,4,5,3,2,1,0:T(1,128)S(1)}, f32[4,2,3,3,1,2,256]{6,4,5,3,2,1,0:T(1,128)S(1)}, u32[]{:S(2)}, u32[]{:S(2)}) collective-permute-start(f32[4,2,3,3,1,2,256]{6,4,5,3,2,1,0:T(1,128)S(1)} %get-tuple-element.349), channel_id=1, source_target_pairs={{8,0},{16,8},{24,16},{0,24},{9,1},{17,9},{25,17},{1,25},{10,2},{18... | collective-permute-start | bytes 442376 | tf_op jit(solution)/shard_map/ppermute | solution.py:24
  19.0 2.4 %collective-permute-done.9 = f32[2,2,4,3,4,1,2,64]{7,6,5,4,3,2,0,1:T(2,128)S(1)} collective-permute-done((f32[2,2,4,3,4,1,2,64]{7,6,5,4,3,2,0,1:T(2,128)S(1)}, f32[2,2,4,3,4,1,2,64]{7,6,5,4,3,2,0,1:T(2,128)S(1)}, u32[]{:S(2)}, u32[]{:S(2)}) %collective-permute-start.9) | collective-permute-done | bytes 98336 | tf_op jit(solution)/shard_map/ppermute | solution.py:24
  21.5 3.4 %collective-permute-done.8 = f32[2,2,4,3,4,1,2,64]{7,6,5,4,3,2,0,1:T(2,128)S(1)} collective-permute-done((f32[2,2,4,3,4,1,2,64]{7,6,5,4,3,2,0,1:T(2,128)S(1)}, f32[2,2,4,3,4,1,2,64]{7,6,5,4,3,2,0,1:T(2,128)S(1)}, u32[]{:S(2)}, u32[]{:S(2)}) %collective-permute-start.8) | collective-permute-done | bytes 98336 | tf_op jit(solution)/shard_map/ppermute | solution.py:23
  27.2 0.9 fusion.74
  28.1 2.4 %collective-permute-start.5 = (f32[4,2,3,3,4,1,256]{6,4,5,3,2,1,0:T(4,128)}, f32[4,2,3,3,4,1,256]{6,4,5,3,2,1,0:T(4,128)}, u32[]{:S(2)}, u32[]{:S(2)}) collective-permute-start(f32[4,2,3,3,4,1,256]{6,4,5,3,2,1,0:T(4,128)} %get-tuple-element.202), channel_id=1, source_target_pairs={{2,0},{4,2},{6,4},{0,6},{3,1},{5,3},{7,5},{1,7},{10,8},{12,10},{14... | collective-permute-start | bytes 884744 | tf_op jit(solution)/shard_map/ppermute | solution.py:24
  30.5 1.3 %maximum_multiply_fusion = f32[2,2,4,3,4,4,4,64]{7,6,5,4,3,2,0,1:T(4,128)S(1)} fusion(f32[2,2,4,3,4,4,1,64]{7,6,5,4,3,2,0,1:T(1,128)S(1)} %collective-permute-done.11, f32[2,2,4,3,4,1,2,64]{7,6,5,4,3,2,0,1:T(2,128)S(1)} %collective-permute-done.9, f32[2,2,4,3,4,2,2,64]{7,6,5,4,3,2,0,1:T(2,128)S(1)} %constant_dynamic-update-slice_fusion, ...), kind=kLoop, calls=%fused_computation | loop fusion | flops 983040 | bytes 1572880 | tf_op jit(solution)/shard_map/mul | solution.py:207
  37.5 0.8 collective-permute-done.5
  38.3 5.7 %collective-permute-done.4 = f32[4,2,3,3,4,1,256]{6,4,5,3,2,1,0:T(4,128)} collective-permute-done((f32[4,2,3,3,4,1,256]{6,4,5,3,2,1,0:T(4,128)}, f32[4,2,3,3,4,1,256]{6,4,5,3,2,1,0:T(4,128)}, u32[]{:S(2)}, u32[]{:S(2)}) %collective-permute-start.4) | collective-permute-done | bytes 294944 | tf_op jit(solution)/shard_map/ppermute | solution.py:23
  44.0 1.8 %pad_maximum_fusion = f32[4,2,3,3,4,4,256]{6,4,5,3,2,1,0:T(4,128)S(1)} fusion(f32[4,2,3,3,4,1,256]{6,4,5,3,2,1,0:T(4,128)} %collective-permute-done.5, f32[4,2,3,3,1,2,256]{6,4,5,3,2,1,0:T(1,128)S(1)} %collective-permute-done.3, f32[4,2,3,3,2,2,64]{6,4,5,3,2,1,0:T(2,128)S(1)} %collective-permute-done.1, f32[4,2,3,3,2,2,128]{6,4,5,3,2,1,0:T(2,128)S(1)} %copy.458, ...), kind=kLoop, calls=%fused_computation.1 | loop fusion | flops 1769472 | bytes 2359296 | tf_op jit(solution)/shard_map/concatenate | solution.py:25
  46.1 0.9 %slice_bitcast_fusion.112 = (f32[3,3,2,2,128]{4,2,3,0,1:T(2,128)S(1)}, f32[3,3,2,2,128]{4,2,3,0,1:T(2,128)S(1)}, f32[3,3,2,2,128]{4,2,3,0,1:T(2,128)}, f32[3,3,2...) fusion(f32[2,3,3,4,4,256]{5,3,4,2,1,0:T(4,128)S(1)} %get-tuple-, ...), kind=kLoop, calls=%fused_computation.441 | loop fusion | flops 18432 | bytes 645120 | tf_op jit(solution)/shard_map/transpose | solution.py:127
  47.0 0.9 slice_bitcast_fusion.94
  48.6 0.8 negate_bitcast_fusion.11
  49.3 1.0 %slice_bitcast_fusion.104 = (f32[3,3,2,2,128]{4,2,3,0,1:T(2,128)S(1)}, f32[3,3,2,2,128]{4,2,3,0,1:T(2,128)}, f32[3,3,2,2,128]{4,2,3,0,1:T(2,128)}, f32[3,3,2,2,1...) fusion(f32[2,3,3,4,4,256]{5,3,4,2,1,0:T(4,128)S(1)} %get-tuple-, ...), kind=kLoop, calls=%fused_computation.433 | loop fusion | flops 18432 | bytes 645120 | tf_op jit(solution)/shard_map/transpose | solution.py:127
  50.3 0.8 negate_bitcast_fusion.13
  53.5 1.0 %slice_bitcast_fusion.85 = (f32[3,3,2,2,128]{4,2,3,1,0:T(2,128)}, f32[3,3,2,2,128]{4,2,3,0,1:T(2,128)}, f32[3,3,2,2,128]{4,2,3,0,1:T(2,128)}, f32[3,3,2,2,128]{4...) fusion(f32[2,3,3,4,4,256]{5,3,4,2,1,0:T(4,128)S(1)} %get-tuple-, ...), kind=kLoop, calls=%fused_computation.414 | loop fusion | flops 13824 | bytes 626688 | tf_op jit(solution)/shard_map/mul | solution.py:114
  78.2 1.5 %collective-permute-start.12 = (f32[2,2,4,3,1,2,2,64]{7,6,5,4,3,2,0,1:T(2,128)S(1)}, f32[2,2,4,3,1,2,2,64]{7,6,5,4,3,2,0,1:T(2,128)S(1)}, u32[]{:S(2)}, u32[]{:S(2)}) collective-permute-start(f32[2,2,4,3,1,2,2,64]{7,6,5,4,3,2,0,1:T(2,128)S(1)} %copy.652), channel_id=1, source_target_pairs={{0,24},{8,0},{16,8},{24,16},{1,25},{9,1},{17,9},{25,17},{2,26},{10... | collective-permute-start | bytes 147464 | tf_op jit(solution)/shard_map/ppermute | solution.py:31
  79.7 2.3 %collective-permute-start.13 = (f32[2,2,4,3,2,1,2,64]{7,6,5,4,3,2,0,1:T(2,128)S(1)}, f32[2,2,4,3,2,1,2,64]{7,6,5,4,3,2,0,1:T(2,128)S(1)}, u32[]{:S(2)}, u32[]{:S(2)}) collective-permute-start(f32[2,2,4,3,2,1,2,64]{7,6,5,4,3,2,0,1:T(2,128)S(1)} %copy.654), channel_id=1, source_target_pairs={{0,6},{2,0},{4,2},{6,4},{1,7},{3,1},{5,3},{7,5},{8,14},{10,8},{12,... | collective-permute-start | bytes 147464 | tf_op jit(solution)/shard_map/ppermute | solution.py:31
  82.8 1.2 %add_reduce_fusion.7 = (f32[3,3,2,2,128]{4,3,2,1,0:T(2,128)S(1)}, f32[3,3,2,2,128]{4,3,2,1,0:T(2,128)}, f32[3,3,2,2,128]{4,3,2,1,0:T(2,128)S(1)}, f32[3,3,2,2,12...) fusion(f32[2,4,3,2,2,128]{5,1,4,3,2,0:T(4,128)S(1)} %get-tuple-, ...), kind=kLoop, calls=%fused_computation.31 | loop fusion | flops 1142784 | bytes 638976 | tf_op jit(solution)/shard_map/reduce_sum | solution.py:171
  (538 shorter events, 47.8 us)
Async XLA Ops:
  1.2 14.9 %collective-permute-start.1 = (f32[4,2,3,3,2,2,64]{6,4,5,3,2,1,0:T(2,128)S(1)}, f32[4,2,3,3,2,2,64]{6,4,5,3,2,1,0:T(2,128)S(1)}, u32[]{:S(2)}, u32[]{:S(2)}) collective-permute-start(f32[4,2,3,3,2,2,64]{6,4,5,3,2,1,0:T(2,128)S(1)} %get-tuple-element.359), channel_id=1, source_target_pairs={{1,0},{0,1},{3,2},{2,3},{5,4},{4,5},{7,6},{6,7},{9,8},{8,9},{11,10... | collective-permute-start | bytes 221192 | tf_op jit(solution)/shard_map/ppermute | solution.py:24
  1.8 14.4 %collective-permute-start = (f32[4,2,3,3,2,2,64]{6,4,5,3,2,1,0:T(2,128)S(1)}, f32[4,2,3,3,2,2,64]{6,4,5,3,2,1,0:T(2,128)S(1)}, u32[]{:S(2)}, u32[]{:S(2)}) collective-permute-start(f32[4,2,3,3,2,2,64]{6,4,5,3,2,1,0:T(2,128)S(1)} %get-tuple-element.358), channel_id=1, source_target_pairs={{0,1},{1,0},{2,3},{3,2},{4,5},{5,4},{6,7},{7,6},{8,9},{9,8},{10,11... | collective-permute-start | bytes 221192 | tf_op jit(solution)/shard_map/ppermute | solution.py:23
  3.0 7.5 %collective-permute-start.6 = (f32[2,2,4,3,1,2,2,64]{7,6,5,4,3,2,0,1:T(2,128)S(1)}, f32[2,2,4,3,1,2,2,64]{7,6,5,4,3,2,0,1:T(2,128)S(1)}, u32[]{:S(2)}, u32[]{:S(2)}) collective-permute-start(f32[2,2,4,3,1,2,2,64]{7,6,5,4,3,2,0,1:T(2,128)S(1)} %copy.683), channel_id=1, source_target_pairs={{0,8},{8,16},{16,24},{24,0},{1,9},{9,17},{17,25},{25,1},{2,10},{10... | collective-permute-start | bytes 147464 | tf_op jit(solution)/shard_map/ppermute | solution.py:23
  6.0 6.3 %collective-permute-start.7 = (f32[2,2,4,3,1,2,2,64]{7,6,5,4,3,2,0,1:T(2,128)S(1)}, f32[2,2,4,3,1,2,2,64]{7,6,5,4,3,2,0,1:T(2,128)S(1)}, u32[]{:S(2)}, u32[]{:S(2)}) collective-permute-start(f32[2,2,4,3,1,2,2,64]{7,6,5,4,3,2,0,1:T(2,128)S(1)} %copy.684), channel_id=1, source_target_pairs={{8,0},{16,8},{24,16},{0,24},{9,1},{17,9},{25,17},{1,25},{10,2},{18... | collective-permute-start | bytes 147464 | tf_op jit(solution)/shard_map/ppermute | solution.py:24
  12.5 8.9 %collective-permute-start.9 = (f32[2,2,4,3,4,1,2,64]{7,6,5,4,3,2,0,1:T(2,128)S(1)}, f32[2,2,4,3,4,1,2,64]{7,6,5,4,3,2,0,1:T(2,128)S(1)}, u32[]{:S(2)}, u32[]{:S(2)}) collective-permute-start(f32[2,2,4,3,4,1,2,64]{7,6,5,4,3,2,0,1:T(2,128)S(1)} %get-tuple-element.204), channel_id=1, source_target_pairs={{2,0},{4,2},{6,4},{0,6},{3,1},{5,3},{7,5},{1,7},{10,8},{12,10},{14... | collective-permute-start | bytes 294920 | tf_op jit(solution)/shard_map/ppermute | solution.py:24
  16.2 8.7 %collective-permute-start.8 = (f32[2,2,4,3,4,1,2,64]{7,6,5,4,3,2,0,1:T(2,128)S(1)}, f32[2,2,4,3,4,1,2,64]{7,6,5,4,3,2,0,1:T(2,128)S(1)}, u32[]{:S(2)}, u32[]{:S(2)}) collective-permute-start(f32[2,2,4,3,4,1,2,64]{7,6,5,4,3,2,0,1:T(2,128)S(1)} %get-tuple-element.203), channel_id=1, source_target_pairs={{0,2},{2,4},{4,6},{6,0},{1,3},{3,5},{5,7},{7,1},{8,10},{10,12},{12... | collective-permute-start | bytes 294920 | tf_op jit(solution)/shard_map/ppermute | solution.py:23
  17.0 9.6 %collective-permute-start.3 = (f32[4,2,3,3,1,2,256]{6,4,5,3,2,1,0:T(1,128)S(1)}, f32[4,2,3,3,1,2,256]{6,4,5,3,2,1,0:T(1,128)S(1)}, u32[]{:S(2)}, u32[]{:S(2)}) collective-permute-start(f32[4,2,3,3,1,2,256]{6,4,5,3,2,1,0:T(1,128)S(1)} %get-tuple-element.349), channel_id=1, source_target_pairs={{8,0},{16,8},{24,16},{0,24},{9,1},{17,9},{25,17},{1,25},{10,2},{18... | collective-permute-start | bytes 442376 | tf_op jit(solution)/shard_map/ppermute | solution.py:24
  18.4 8.1 %collective-permute-start.2 = (f32[4,2,3,3,1,2,256]{6,4,5,3,2,1,0:T(1,128)S(1)}, f32[4,2,3,3,1,2,256]{6,4,5,3,2,1,0:T(1,128)S(1)}, u32[]{:S(2)}, u32[]{:S(2)}) collective-permute-start(f32[4,2,3,3,1,2,256]{6,4,5,3,2,1,0:T(1,128)S(1)} %get-tuple-element.348), channel_id=1, source_target_pairs={{0,8},{8,16},{16,24},{24,0},{1,9},{9,17},{17,25},{25,1},{2,10},{10... | collective-permute-start | bytes 442376 | tf_op jit(solution)/shard_map/ppermute | solution.py:23
  25.9 4.5 %collective-permute-start.11 = (f32[2,2,4,3,4,4,1,64]{7,6,5,4,3,2,0,1:T(1,128)S(1)}, f32[2,2,4,3,4,4,1,64]{7,6,5,4,3,2,0,1:T(1,128)S(1)}, u32[]{:S(2)}, u32[]{:S(2)}) collective-permute-start(f32[2,2,4,3,4,4,1,64]{7,6,5,4,3,2,0,1:T(1,128)S(1)} %get-tuple-element.200), channel_id=1, source_target_pairs={{1,0},{0,1},{3,2},{2,3},{5,4},{4,5},{7,6},{6,7},{9,8},{8,9},{11,10... | collective-permute-start | bytes 589832 | tf_op jit(solution)/shard_map/ppermute | solution.py:24
  26.0 4.5 %collective-permute-start.10 = (f32[2,2,4,3,4,4,1,64]{7,6,5,4,3,2,0,1:T(1,128)S(1)}, f32[2,2,4,3,4,4,1,64]{7,6,5,4,3,2,0,1:T(1,128)S(1)}, u32[]{:S(2)}, u32[]{:S(2)}) collective-permute-start(f32[2,2,4,3,4,4,1,64]{7,6,5,4,3,2,0,1:T(1,128)S(1)} %get-tuple-element.199), channel_id=1, source_target_pairs={{0,1},{1,0},{2,3},{3,2},{4,5},{5,4},{6,7},{7,6},{8,9},{9,8},{10,11... | collective-permute-start | bytes 589832 | tf_op jit(solution)/shard_map/ppermute | solution.py:23
  28.1 10.2 %collective-permute-start.5 = (f32[4,2,3,3,4,1,256]{6,4,5,3,2,1,0:T(4,128)}, f32[4,2,3,3,4,1,256]{6,4,5,3,2,1,0:T(4,128)}, u32[]{:S(2)}, u32[]{:S(2)}) collective-permute-start(f32[4,2,3,3,4,1,256]{6,4,5,3,2,1,0:T(4,128)} %get-tuple-element.202), channel_id=1, source_target_pairs={{2,0},{4,2},{6,4},{0,6},{3,1},{5,3},{7,5},{1,7},{10,8},{12,10},{14... | collective-permute-start | bytes 884744 | tf_op jit(solution)/shard_map/ppermute | solution.py:24
  30.5 13.5 %collective-permute-start.4 = (f32[4,2,3,3,4,1,256]{6,4,5,3,2,1,0:T(4,128)}, f32[4,2,3,3,4,1,256]{6,4,5,3,2,1,0:T(4,128)}, u32[]{:S(2)}, u32[]{:S(2)}) collective-permute-start(f32[4,2,3,3,4,1,256]{6,4,5,3,2,1,0:T(4,128)} %get-tuple-element.201), channel_id=1, source_target_pairs={{0,2},{2,4},{4,6},{6,0},{1,3},{3,5},{5,7},{7,1},{8,10},{10,12},{12... | collective-permute-start | bytes 884744 | tf_op jit(solution)/shard_map/ppermute | solution.py:23
  62.3 10.6 %copy-start.29 = (f32[3,3,2,2,128]{4,2,3,1,0:T(2,128)S(1)}, f32[3,3,2,2,128]{4,2,3,1,0:T(2,128)}, u32[]{:S(2)}) copy-start(f32[3,3,2,2,128]{4,2,3,1,0:T(2,128)} %get-tuple-element.291) | copy-start | bytes 55300
  62.4 10.7 %copy-start.15 = (f32[3,3,2,2,128]{4,2,3,0,1:T(2,128)S(1)}, f32[3,3,2,2,128]{4,2,3,0,1:T(2,128)}, u32[]{:S(2)}) copy-start(f32[3,3,2,2,128]{4,2,3,0,1:T(2,128)} %get-tuple-element.308) | copy-start | bytes 55300
  62.4 10.7 %copy-start.27 = (f32[3,3,2,2,128]{4,2,3,0,1:T(2,128)S(1)}, f32[3,3,2,2,128]{4,2,3,0,1:T(2,128)}, u32[]{:S(2)}) copy-start(f32[3,3,2,2,128]{4,2,3,0,1:T(2,128)} %get-tuple-element.287) | copy-start | bytes 55300
  62.7 10.5 %copy-start.21 = (f32[3,3,2,2,128]{4,2,3,1,0:T(2,128)S(1)}, f32[3,3,2,2,128]{4,2,3,1,0:T(2,128)}, u32[]{:S(2)}) copy-start(f32[3,3,2,2,128]{4,2,3,1,0:T(2,128)} %get-tuple-element.292) | copy-start | bytes 55300
  62.9 11.3 %copy-start.19 = (f32[3,3,2,2,128]{4,2,3,0,1:T(2,128)S(1)}, f32[3,3,2,2,128]{4,2,3,0,1:T(2,128)}, u32[]{:S(2)}) copy-start(f32[3,3,2,2,128]{4,2,3,0,1:T(2,128)} %get-tuple-element.532) | copy-start | bytes 55300
  63.2 13.5 %copy-start.46 = (f32[3,3,2,2,128]{4,2,3,1,0:T(2,128)S(1)}, f32[3,3,2,2,128]{4,2,3,1,0:T(2,128)}, u32[]{:S(2)}) copy-start(f32[3,3,2,2,128]{4,2,3,1,0:T(2,128)} %get-tuple-element.257) | copy-start | bytes 55300
  64.0 11.9 %copy-start.48 = (f32[3,3,2,2,128]{4,2,3,1,0:T(2,128)S(1)}, f32[3,3,2,2,128]{4,2,3,1,0:T(2,128)}, u32[]{:S(2)}) copy-start(f32[3,3,2,2,128]{4,2,3,1,0:T(2,128)} %get-tuple-element.268) | copy-start | bytes 55300
  64.1 11.8 %copy-start.49 = (f32[3,3,2,2,128]{4,2,3,1,0:T(2,128)S(1)}, f32[3,3,2,2,128]{4,2,3,1,0:T(2,128)}, u32[]{:S(2)}) copy-start(f32[3,3,2,2,128]{4,2,3,1,0:T(2,128)} %get-tuple-element.270) | copy-start | bytes 55300
  64.2 10.9 %copy-start.51 = (f32[3,3,2,2,128]{4,2,3,1,0:T(2,128)S(1)}, f32[3,3,2,2,128]{4,2,3,1,0:T(2,128)}, u32[]{:S(2)}) copy-start(f32[3,3,2,2,128]{4,2,3,1,0:T(2,128)} %get-tuple-element.269) | copy-start | bytes 55300
  78.2 10.2 %collective-permute-start.12 = (f32[2,2,4,3,1,2,2,64]{7,6,5,4,3,2,0,1:T(2,128)S(1)}, f32[2,2,4,3,1,2,2,64]{7,6,5,4,3,2,0,1:T(2,128)S(1)}, u32[]{:S(2)}, u32[]{:S(2)}) collective-permute-start(f32[2,2,4,3,1,2,2,64]{7,6,5,4,3,2,0,1:T(2,128)S(1)} %copy.652), channel_id=1, source_target_pairs={{0,24},{8,0},{16,8},{24,16},{1,25},{9,1},{17,9},{25,17},{2,26},{10... | collective-permute-start | bytes 147464 | tf_op jit(solution)/shard_map/ppermute | solution.py:31
  79.7 9.2 %collective-permute-start.13 = (f32[2,2,4,3,2,1,2,64]{7,6,5,4,3,2,0,1:T(2,128)S(1)}, f32[2,2,4,3,2,1,2,64]{7,6,5,4,3,2,0,1:T(2,128)S(1)}, u32[]{:S(2)}, u32[]{:S(2)}) collective-permute-start(f32[2,2,4,3,2,1,2,64]{7,6,5,4,3,2,0,1:T(2,128)S(1)} %copy.654), channel_id=1, source_target_pairs={{0,6},{2,0},{4,2},{6,4},{1,7},{3,1},{5,3},{7,5},{8,14},{10,8},{12,... | collective-permute-start | bytes 147464 | tf_op jit(solution)/shard_map/ppermute | solution.py:31
  82.1 7.3 %collective-permute-start.14 = (f32[2,2,4,3,2,2,1,64]{7,6,5,4,3,2,0,1:T(1,128)S(1)}, f32[2,2,4,3,2,2,1,64]{7,6,5,4,3,2,0,1:T(1,128)S(1)}, u32[]{:S(2)}, u32[]{:S(2)}) collective-permute-start(f32[2,2,4,3,2,2,1,64]{7,6,5,4,3,2,0,1:T(1,128)S(1)} %copy.656), channel_id=1, source_target_pairs={{0,1},{1,0},{2,3},{3,2},{4,5},{5,4},{6,7},{7,6},{8,9},{9,8},{10,11... | collective-permute-start | bytes 147464 | tf_op jit(solution)/shard_map/ppermute | solution.py:31
  (63 other events, 401.5 us)
where the time goes:
time: 94.3 us; the launch traced here: 93.2 us
  local copies, waits for them, and re-layouts  30.4 us (32%)
  other arithmetic  27.6 us (29%)
  starting transfers between devices  17.2 us (18%)
  waiting for transfers between devices  14.5 us (15%)
  between operations  3.44 us (4%)
    ppermute x6, waiting for transfers between devices, padded_2(): before = lax.ppermute(last, axis, up)  9.57 us
    ppermute x6, starting transfers between devices, padded_2(): after = lax.ppermute(initial, axis, down)  9.15 us
    transpose x47, local copies, waits for them, and re-layouts, dagger(): jnp.swapaxes(matrix[0], 0, 1)  6.7 us
    ppermute x6, waiting for transfers between devices, padded_2(): after = lax.ppermute(initial, axis, down)  4.93 us
    reduce_sum x33, other arithmetic, matrix_product(): jnp.sum(left_real[:, :, None] * right_real[None] - left_imaginary[:, :, N...  4.49 us
    ppermute x6, starting transfers between devices, padded_2(): before = lax.ppermute(last, axis, up)  4.13 us
    ppermute x3, starting transfers between devices, shifted(): lax.ppermute(x, axis, [(i, (i + by) % length) for i in range(length)])  3.87 us
    neg x6, other arithmetic, dagger(): -jnp.swapaxes(matrix[1], 0, 1)  3.43 us
  transfers between devices with their start and end apart: 15, of which 6 were waited for; matrix products, arithmetic and copies ran while one was open for 23% of the time, Pallas kernels for 0%

commit v1 on v0

v1 whole, which is shorter than its diff:
```python
import functools

import jax
import jax.numpy as jnp
from jax import lax
from jax.experimental import pallas as pl
from jax.experimental.pallas import tpu as pltpu
from jax.sharding import PartitionSpec as P

Y_LEN = 64
HOPPING = 0.125
PLAQUETTE = 0.5
AXES = ("ta", "gz", "xy")
MESH = pl.DeviceIdType.MESH

SIGMA = (
    ((0, 0), (1, 0)),
    ((0, 1), (1, 3)),
    ((1, 1), (0, 1)),
    ((1, 2), (0, 0)),
)


def phased(value, power):
    re, im = value
    return ((re, im), (-im, re), (-re, -im), (im, -re))[power % 4]


def added(a, b, sign):
    if sign > 0:
        return a[0] + b[0], a[1] + b[1]
    return a[0] - b[0], a[1] - b[1]


def half(x, mu, sign):
    rows = []
    for s in range(2):
        column, power = SIGMA[mu][s]
        lower = phased((x[0][2 + column], x[1][2 + column]), power)
        rows.append(added((x[0][s], x[1][s]), lower, sign))
    return jnp.stack([rows[0][0], rows[1][0]]), jnp.stack([rows[0][1], rows[1][1]])


def full_rows(h, mu, sign):
    lower = [None, None]
    for s in range(2):
        column, power = SIGMA[mu][s]
        lower[column] = phased((h[0][s], h[1][s]), (-power if sign > 0 else 2 - power))
    return [(h[0][0], h[1][0]), (h[0][1], h[1][1])] + lower


def product(left, right, left_dagger=False, right_dagger=False):
    re = im = None
    for k in range(3):
        ar, ai = (left[0][k], left[1][k]) if left_dagger else (left[0][:, k], left[1][:, k])
        br, bi = (right[0][:, k], right[1][:, k]) if right_dagger else (right[0][k], right[1][k])
        ar, ai, br, bi = ar[:, None], ai[:, None], br[None], bi[None]
        rr, ii, ri, ir = ar * br, ai * bi, ar * bi, ai * br
        same = left_dagger == right_dagger
        re_k = rr - ii if same else rr + ii
        if left_dagger:
            im_k = -(ri + ir) if right_dagger else ri - ir
        else:
            im_k = ir - ri if right_dagger else ri + ir
        re = re_k if re is None else re + re_k
        im = im_k if im is None else im + im_k
    return re, im


def colour(u, h, dagger=False):
    re = im = None
    for k in range(3):
        ur, ui = (u[0][k], u[1][k]) if dagger else (u[0][:, k], u[1][:, k])
        ur, ui = ur[None], ui[None]
        hr, hi = h[0][:, k][:, None], h[1][:, k][:, None]
        if dagger:
            re_k, im_k = ur * hr + ui * hi, ur * hi - ui * hr
        else:
            re_k, im_k = ur * hr - ui * hi, ur * hi + ui * hr
        re = re_k if re is None else re + re_k
        im = im_k if im is None else im + im_k
    return re, im


def outer(f, g):
    re = im = None
    for s in range(2):
        fr, fi = f[0][s][:, None], f[1][s][:, None]
        gr, gi = g[0][s][None], g[1][s][None]
        re_s, im_s = fr * gr + fi * gi, fi * gr - fr * gi
        re = re_s if re is None else re + re_s
        im = im_s if im is None else im + im_s
    return re, im


def nine(m, scale):
    re, im = m
    pairs = ((0, 1), (0, 2), (1, 2))
    parts = [(re[i, j] - re[j, i]) * (0.5 * scale) for i, j in pairs]
    parts += [(im[i, j] + im[j, i]) * (0.5 * scale) for i, j in pairs]
    parts += [im[i, i] * scale for i in range(3)]
    return jnp.stack(parts)


def roll(value, by):
    lanes = value.shape[-1]
    return pltpu.roll(value, by % lanes, value.ndim - 1)


def y_shift(value, stride):
    lanes = value.shape[-1]
    at = lax.broadcasted_iota(jnp.int32, value.shape, value.ndim - 1) % Y_LEN
    if stride > 0:
        return jnp.where(at == Y_LEN - 1, roll(value, Y_LEN - 1), roll(value, lanes - 1))
    return jnp.where(at == 0, roll(value, lanes - Y_LEN + 1), roll(value, 1))


def r_ahead(here, ahead):
    lane = lax.broadcasted_iota(jnp.int32, here.shape, here.ndim - 1)
    return roll(jnp.where(lane < Y_LEN, ahead, here), here.shape[-1] - Y_LEN)


def r_behind(here, behind):
    lanes = here.shape[-1]
    lane = lax.broadcasted_iota(jnp.int32, here.shape, here.ndim - 1)
    return roll(jnp.where(lane >= lanes - Y_LEN, behind, here), Y_LEN)


def offsets(sizes):
    t, z, r = (1, 0, 0), (0, 1, 0), (0, 0, 1)
    steps = [t, z, r]
    steps += [(1, -1, 0), (1, 0, -1), (0, 1, -1)]
    both = steps + [tuple(-c for c in step) for step in steps]
    unique = []
    for step in both:
        seat = tuple(c % n for c, n in zip(step, sizes))
        if seat not in unique:
            unique.append(seat)
    return unique


LOCAL_COPIES = 64
REMOTE_COPIES = 96


def kernel(sizes, block, links, solutions, force, *refs):
    (ul, utp, utm, uzp, uzm, urf, urb, urp, urm, uyp, uym, edges, far, xs,
     xtp, xtm, xzp, xzm, xrf, xrb, ys, hy, hyn, ws, fs, gs, local, sends, recvs) = refs
    blocks_t, blocks_z = block
    rows, lanes = ul.shape[-2:]
    solves = xs.shape[-2] // rows
    last_t, last_z = blocks_t - 1, blocks_z - 1
    one_ring = sizes[2] == 2
    if one_ring:
        urb, xrb = urf, xrf
    me = [lax.axis_index(axis) for axis in AXES]

    def seat(step):
        return {
            axis: m if c % n == 0 else lax.rem(m + (c % n), n)
            for axis, m, c, n in zip(AXES, me, step, sizes)
        }

    every_t, every_z = (0, blocks_t), (0, blocks_z)

    def runs(box_t, box_z):
        (t, many_t), (z, many_z) = box_t, box_z
        if many_z == blocks_z:
            return [(t * blocks_z, many_t * blocks_z)]
        return [((t + k) * blocks_z + z, many_z) for k in range(many_t)]

    head_t, tail_t, zero, edge_t = (0, last_t), (1, last_t), (0, 1), (last_t, 1)
    head_z, tail_z, edge_z = (0, last_z), (1, last_z), (last_z, 1)

    locals_, remotes = [], []

    def bring(source, target):
        copy = pltpu.make_async_copy(source, target, local.at[len(locals_)])
        copy.start()
        locals_.append(copy)

    def send(source, target, step):
        k = len(remotes)
        copy = pltpu.make_async_remote_copy(
            src_ref=source, dst_ref=target, send_sem=sends.at[k], recv_sem=recvs.at[k],
            device_id=seat(step), device_id_type=MESH,
        )
        copy.start()
        remotes.append(copy)

    def boxes(source, from_box, target, to_box, lead, one):
        everything = (slice(None),) * lead
        for (a, n), (b, _) in zip(runs(*from_box), runs(*to_box)):
            one(source.at[(*everything, pl.ds(a, n))], target.at[(*everything, pl.ds(b, n))])

    def spinor_boxes(source, from_box, target, to_box, lead, one):
        everything = (slice(None),) * lead
        for s in range(solves):
            for (a, n), (b, _) in zip(runs(*from_box), runs(*to_box)):
                one(
                    source.at[(*everything, pl.ds(s * rows + a, n))],
                    target.at[(*everything, pl.ds(s * rows + b, n))],
                )

    bring(links, ul)
    for n in range(solves):
        bring(solutions.at[n], xs.at[:, :, :, pl.ds(n * rows, rows)])
    first_locals = len(locals_)
    boxes(links, (tail_t, every_z), utp, (head_t, every_z), 4, bring)
    boxes(links, (head_t, every_z), utm, (tail_t, every_z), 4, bring)
    boxes(links, (every_t, tail_z), uzp, (every_t, head_z), 4, bring)
    boxes(links, (every_t, head_z), uzm, (every_t, tail_z), 4, bring)
    boxes(links.at[1], (tail_t, head_z), edges.at[0], (head_t, tail_z), 3, bring)
    boxes(links.at[0], (head_t, tail_z), edges.at[1], (tail_t, head_z), 3, bring)

    barrier = pltpu.get_barrier_semaphore()
    peers = offsets(sizes)
    for step in peers:
        pl.semaphore_signal(barrier, inc=1, device_id=seat(step), device_id_type=MESH)
    for copy in locals_[:first_locals]:
        copy.wait()
    pl.semaphore_wait(barrier, len(peers))

    t_ahead, t_behind, z_ahead, z_behind = (1, 0, 0), (-1, 0, 0), (0, 1, 0), (0, -1, 0)
    r_next, r_prev = (0, 0, 1), (0, 0, -1)

    def sent(source, from_t, from_z, target, to_t, to_z, lead, step):
        boxes(source, (from_t, from_z), target, (to_t, to_z), lead,
              lambda a, b: send(a, b, step))

    def sent_spinor(source, from_t, from_z, target, to_t, to_z, lead, step):
        spinor_boxes(source, (from_t, from_z), target, (to_t, to_z), lead,
                     lambda a, b: send(a, b, step))

    sent_spinor(xs, zero, every_z, xtp, edge_t, every_z, 3, t_behind)
    sent_spinor(xs, edge_t, every_z, xtm, zero, every_z, 3, t_ahead)
    sent_spinor(xs, every_t, zero, xzp, every_t, edge_z, 3, z_behind)
    sent_spinor(xs, every_t, edge_z, xzm, every_t, zero, 3, z_ahead)
    sent(ul.at[0], edge_t, every_z, utm.at[0], zero, every_z, 3, t_ahead)
    sent(ul.at[1], every_t, edge_z, uzm.at[1], every_t, zero, 3, z_ahead)
    send(xs, xrf, r_prev)
    if not one_ring:
        send(xs, xrb, r_next)
    send(ul.at[2], urb.at[2], r_prev if one_ring else r_next)
    first_remotes = len(remotes)
    later, other = pl.ds(1, 3), pl.ds(2, 2)
    sent(ul.at[later], zero, every_z, utp.at[later], edge_t, every_z, 4, t_behind)
    sent(ul.at[later], edge_t, every_z, utm.at[later], zero, every_z, 4, t_ahead)
    sent(ul.at[0], every_t, zero, uzp.at[0], every_t, edge_z, 3, z_behind)
    sent(ul.at[other], every_t, zero, uzp.at[other], every_t, edge_z, 4, z_behind)
    sent(ul.at[0], every_t, edge_z, uzm.at[0], every_t, zero, 3, z_ahead)
    sent(ul.at[other], every_t, edge_z, uzm.at[other], every_t, zero, 4, z_ahead)
    sent(ul.at[1], tail_t, edge_z, edges.at[0], head_t, zero, 3, z_ahead)
    sent(ul.at[1], zero, edge_z, edges.at[0], edge_t, zero, 3, (-1, 1, 0))
    sent(ul.at[1], zero, head_z, edges.at[0], edge_t, tail_z, 3, t_behind)
    sent(ul.at[0], edge_t, tail_z, edges.at[1], zero, head_z, 3, t_ahead)
    sent(ul.at[0], edge_t, zero, edges.at[1], zero, edge_z, 3, (1, -1, 0))
    sent(ul.at[0], head_t, zero, edges.at[1], tail_t, edge_z, 3, z_behind)
    sent(ul.at[2], zero, every_z, far.at[0], edge_t, every_z, 3, (-1, 0, 1))
    sent(ul.at[0], edge_t, every_z, far.at[1], zero, every_z, 3, (1, 0, -1))
    sent(ul.at[2], every_t, zero, far.at[2], every_t, edge_z, 3, (0, -1, 1))
    sent(ul.at[1], every_t, edge_z, far.at[3], every_t, zero, 3, (0, 1, -1))
    sent(ul.at[2], tail_t, every_z, far.at[0], head_t, every_z, 3, r_next)
    sent(ul.at[0], head_t, every_z, far.at[1], tail_t, every_z, 3, r_prev)
    sent(ul.at[2], every_t, tail_z, far.at[2], every_t, head_z, 3, r_next)
    sent(ul.at[1], every_t, head_z, far.at[3], every_t, tail_z, 3, r_prev)
    send(ul.at[pl.ds(0, 2)], urf.at[pl.ds(0, 2)], r_prev)
    send(ul.at[3], urf.at[3], r_prev)
    if not one_ring:
        send(ul.at[pl.ds(0, 2)], urb.at[pl.ds(0, 2)], r_next)
        send(ul.at[3], urb.at[3], r_next)
    link_remotes = len(remotes)
    spinor_boxes(xs, (tail_t, every_z), xtp, (head_t, every_z), 3, bring)
    spinor_boxes(xs, (head_t, every_z), xtm, (tail_t, every_z), 3, bring)
    spinor_boxes(xs, (every_t, tail_z), xzp, (every_t, head_z), 3, bring)
    spinor_boxes(xs, (every_t, head_z), xzm, (every_t, tail_z), 3, bring)

    def spinor(ref):
        return ref[0], ref[1]

    def gauge(ref, mu):
        return ref[mu, 0], ref[mu, 1]

    def put(ref, mu, value):
        ref[mu, 0], ref[mu, 1] = value

    def doubled(ref, mu):
        re, im = gauge(ref, mu)
        return jnp.concatenate([re] * solves, 2), jnp.concatenate([im] * solves, 2)

    def both(f, *values):
        return tuple(f(*parts) for parts in zip(*values))

    index = lax.broadcasted_iota(jnp.int32, (solves * rows, lanes), 0)
    index = (index // blocks_z) % blocks_t
    wraps_ahead = (index == last_t) & (me[0] == sizes[0] - 1)
    wraps_behind = (index == 0) & (me[0] == 0)
    ahead_sign = jnp.where(wraps_ahead, -1.0, 1.0)
    behind_sign = jnp.where(wraps_behind, -1.0, 1.0)

    def signed(h, sign):
        return both(lambda v: v * sign, h)

    def y_up(value):
        return both(lambda v: y_shift(v, 1), value)

    def y_down(value):
        return both(lambda v: y_shift(v, -1), value)

    for mu in range(4):
        here = gauge(ul, mu)
        if mu < 3:
            put(uyp, mu, y_up(here))
        put(uym, mu, y_down(here))

    for copy in locals_[first_locals:]:
        copy.wait()
    for copy in remotes[:first_remotes]:
        copy.wait_recv()

    put(urm, 2, both(r_behind, gauge(ul, 2), gauge(urb, 2)))

    x = spinor(xs)
    total = [None] * 4

    def gather(w, mu, sign):
        for k, row in enumerate(full_rows(w, mu, sign)):
            total[k] = row if total[k] is None else added(total[k], row, 1)

    for mu in range(4):
        if mu == 0:
            ahead = signed(half(spinor(xtp), mu, -1), ahead_sign)
            behind = signed(half(spinor(xtm), mu, 1), behind_sign)
        elif mu == 1:
            ahead, behind = half(spinor(xzp), mu, -1), half(spinor(xzm), mu, 1)
        elif mu == 2:
            ahead = both(r_ahead, half(x, mu, -1), half(spinor(xrf), mu, -1))
            behind = both(r_behind, half(x, mu, 1), half(spinor(xrb), mu, 1))
        else:
            ahead, behind = y_up(half(x, mu, -1)), y_down(half(x, mu, 1))
        forward = colour(doubled(ul, mu), ahead)
        put(ws, mu, forward)
        gather(forward, mu, -1)
        gather(colour(doubled((utm, uzm, urm, uym)[mu], mu), behind, True), mu, 1)
    y = (
        jnp.stack([x[0][k] - HOPPING * total[k][0] for k in range(4)]),
        jnp.stack([x[1][k] - HOPPING * total[k][1] for k in range(4)]),
    )
    ys[0], ys[1] = y
    for mu in range(3):
        put(hy, mu, half(y, mu, 1))

    sent_spinor(hy.at[0], zero, every_z, hyn.at[0], edge_t, every_z, 3, t_behind)
    sent_spinor(hy.at[1], every_t, zero, hyn.at[1], every_t, edge_z, 3, z_behind)
    send(hy.at[2], hyn.at[2], r_prev)
    staged = len(locals_)
    spinor_boxes(hy.at[0], (tail_t, every_z), hyn.at[0], (head_t, every_z), 3, bring)
    spinor_boxes(hy.at[1], (every_t, tail_z), hyn.at[1], (every_t, head_z), 3, bring)

    for copy in remotes[first_remotes:link_remotes]:
        copy.wait_recv()

    for mu in (0, 1, 3):
        here = gauge(ul, mu)
        put(urp, mu, both(r_ahead, here, gauge(urf, mu)))
        put(urm, mu, both(r_behind, here, gauge(urb, mu)))
    put(edges, 2, both(r_behind, gauge(utp, 2), gauge(far, 0)))
    put(edges, 3, both(r_ahead, gauge(utm, 0), gauge(far, 1)))
    put(edges, 4, both(r_behind, gauge(uzp, 2), gauge(far, 2)))
    put(edges, 5, both(r_ahead, gauge(uzm, 1), gauge(far, 3)))
    put(edges, 6, y_down(gauge(utp, 3)))
    put(edges, 7, y_up(gauge(utm, 0)))
    put(edges, 8, y_down(gauge(uzp, 3)))
    put(edges, 9, y_up(gauge(uzm, 1)))
    put(edges, 10, y_down(gauge(urp, 3)))
    put(edges, 11, y_up(gauge(urm, 2)))

    slot_of = {(0, 1): 0, (1, 0): 1, (0, 2): 2, (2, 0): 3, (1, 2): 4, (2, 1): 5,
               (0, 3): 6, (3, 0): 7, (1, 3): 8, (3, 1): 9, (2, 3): 10, (3, 2): 11}
    plus = (utp, uzp, urp, uyp)
    minus = (utm, uzm, urm, uym)

    def paired(one, two):
        return both(lambda p, q: jnp.concatenate([p, q], 2), one, two)

    def swapped(value):
        return both(lambda v: jnp.concatenate([v[:, :, rows:], v[:, :, :rows]], 2), value)

    planes = [(mu, nu) for mu in range(4) for nu in range(mu + 1, 4)]
    for k, (mu, nu) in enumerate(planes):
        here = paired(gauge(ul, mu), gauge(ul, nu))
        ahead = paired(gauge(plus[mu], nu), gauge(plus[nu], mu))
        walk = product(here, ahead)
        upper = product(walk, swapped(walk), right_dagger=True)
        corner = paired(gauge(edges, slot_of[mu, nu]), gauge(edges, slot_of[nu, mu]))
        side = paired(gauge(minus[nu], mu), gauge(minus[mu], nu))
        back = paired(gauge(minus[nu], nu), gauge(minus[mu], mu))
        lower = product(
            product(here, corner, right_dagger=True), product(side, back, left_dagger=True)
        )
        fs[k] = nine(added(upper, lower, 1), PLAQUETTE)

    for copy in locals_[staged:]:
        copy.wait()
    for copy in remotes[link_remotes:]:
        copy.wait_recv()

    x = spinor(xs)
    y = spinor(ys)
    for mu in range(4):
        if mu == 3:
            ahead = y_up(half(y, 3, 1))
        elif mu == 2:
            ahead = both(r_ahead, gauge(hy, 2), gauge(hyn, 2))
        else:
            ahead = gauge(hyn, mu)
            if mu == 0:
                ahead = signed(ahead, ahead_sign)
        moved = colour(doubled(ul, mu), ahead)
        term = added(outer(gauge(ws, mu), half(y, mu, -1)), outer(moved, half(x, mu, 1)), 1)
        gs[mu] = nine(term, HOPPING)
        parts = gs[mu, :, pl.ds(0, rows)]
        for n in range(1, solves):
            parts = parts + gs[mu, :, pl.ds(n * rows, rows)]
        for k, plane in enumerate(planes):
            if mu in plane:
                parts = parts + fs[k, :, pl.ds(plane.index(mu) * rows, rows)]
        third = (parts[6] + parts[7] + parts[8]) / 3.0
        for k, (i, j) in enumerate(((0, 1), (0, 2), (1, 2))):
            force[mu, 0, i, j] = parts[k]
            force[mu, 0, j, i] = -parts[k]
            force[mu, 1, i, j] = parts[3 + k]
            force[mu, 1, j, i] = parts[3 + k]
        for i in range(3):
            force[mu, 0, i, i] = jnp.zeros_like(third)
            force[mu, 1, i, i] = parts[6 + i] - third

    for copy in remotes:
        copy.wait_send()


def on_device(sizes, links, solutions):
    whole = links.shape
    lanes = whole[-1]
    block = whole[4:6]
    rows = block[0] * block[1]
    links = links.reshape(*whole[:4], rows, lanes)
    n, c, s, a = solutions.shape[:4]
    solutions = solutions.reshape(n, c, s, a, rows, lanes)

    def vmem(*shape):
        return pltpu.VMEM(shape, jnp.float32)

    u = vmem(*links.shape)
    x = vmem(c, s, a, n * rows, lanes)
    unused = vmem(8, lanes) if sizes[2] == 2 else None
    small = links.shape[1:]
    h = vmem(3, c, 2, a, n * rows, lanes)
    out = pl.pallas_call(
        functools.partial(kernel, sizes, block),
        out_shape=jax.ShapeDtypeStruct(links.shape, jnp.float32),
        in_specs=[pl.BlockSpec(memory_space=pl.ANY)] * 2,
        out_specs=pl.BlockSpec(memory_space=pltpu.VMEM),
        scratch_shapes=[u] * 6 + [unused or u] + [u] * 4 + [vmem(12, *small), vmem(4, *small)]
        + [x] * 6 + [unused or x] + [x, h, h]
        + [vmem(4, c, 2, a, n * rows, lanes), vmem(6, 9, 2 * rows, lanes),
           vmem(4, 9, n * rows, lanes)]
        + [pltpu.SemaphoreType.DMA((LOCAL_COPIES,)), pltpu.SemaphoreType.DMA((REMOTE_COPIES,)),
           pltpu.SemaphoreType.DMA((REMOTE_COPIES,))],
        compiler_params=pltpu.CompilerParams(collective_id=0, has_side_effects=True),
    )(links, solutions)
    return out.reshape(whole)


def solution(mesh):
    sizes = tuple(mesh.shape[axis] for axis in AXES)
    spec = P(None, None, None, None, *AXES)
    return jax.shard_map(
        functools.partial(on_device, sizes), mesh=mesh, in_specs=(spec, spec), out_specs=spec,
        check_vma=False,
    )
```

time: 94.3 us -> 21.1 us (0.22); the launches traced: 93.2 us -> 20.9 us
  local copies, waits for them, and re-layouts: 30.4 us -> 1.59 us
  other arithmetic: 27.6 us -> 0 us
  Pallas kernels: 0 us -> 19.3 us
  starting transfers between devices: 17.2 us -> 0 us
  waiting for transfers between devices: 14.5 us -> 0 us
  between operations: 3.44 us -> 0.01 us
    pallas_call x0 -> x1, Pallas kernels: none -> 19.3 us  [on_device(): pl.pallas_call(functools.partial(kernel, sizes, block), out_shape=jax.Sha...]
    ppermute x15 -> x0, starting transfers between devices: 17.2 us -> none  [the longest x6 9.15 us: padded_2(): after = lax.ppermute(initial, axis, down)]
    ppermute x15 -> x0, waiting for transfers between devices: 14.5 us -> none  [the longest x6 9.57 us: padded_2(): before = lax.ppermute(last, axis, up)]
    reduce_sum x43 -> x0, other arithmetic: 7.3 us -> none  [the longest x33 4.49 us: matrix_product(): jnp.sum(left_real[:, :, None] * right_real[None] - left_imaginary[:, :, N...]
    transpose x47 -> x0, local copies, waits for them, and re-layouts: 6.7 us -> none  [dagger(): jnp.swapaxes(matrix[0], 0, 1)]
    slice x22 -> x0, local copies, waits for them, and re-layouts: 6.28 us -> none  [the longest x5 2.17 us: padded_2(): last = lax.slice_in_dim(x, length - width, length, axis=dim)]
    mul x30 -> x0, local copies, waits for them, and re-layouts: 5.01 us -> none  [the longest x16 2.9 us: matrix_product(): left_real[:, :, None] * right_real[None]]
    concatenate x9 -> x0, other arithmetic: 4.59 us -> none  [the longest x4 3.41 us: padded_2(): x = jnp.concatenate([before, x, after], axis=dim)]
  transfers between devices with their start and end apart: 15 -> 0, of which waited for: 6 -> 0; matrix products, arithmetic and copies ran while one was open for 23% -> 0% of each run, Pallas kernels for 0% -> 0%
where the time goes in v1:
time: 21.1 us; the launch traced here: 20.9 us
  Pallas kernels  19.3 us (91%)
  local copies, waits for them, and re-layouts  1.59 us (8%)
    pallas_call x1, Pallas kernels, on_device(): pl.pallas_call(functools.partial(kernel, sizes, block), out_shape=jax.Sha...  19.3 us
    unnamed x1, local copies, waits for them, and re-layouts  1.59 us

profile of v1, /device:TPU:0, one launch (start us, length us, event | category | flops | bytes accessed | tf_op | source)
XLA Modules:
  0.0 20.9 jit_solution(8538757902587061729)
XLA Ops:
  0.0 19.3 %shard_map.28 = f32[4,2,3,3,4,128]{5,4,3,2,1,0:T(4,128)} custom-call(f32[4,2,3,3,4,128]{5,4,3,2,1,0:T(4,128)} %bitcast.4, f32[2,2,4,3,4,128]{5,4,3,2,1,0:T(4,128)} %bitcast.5), custom_call_target="tpu_custom_call" | custom-call | tf_op jit(solution)/shard_map/pallas_call | solution.py:459
  19.3 1.6 %copy.4 = f32[4,2,3,3,2,2,128]{6,5,4,3,2,1,0:T(2,128)} copy(f32[4,2,3,3,2,2,128]{6,5,4,3,2,1,0:T(2,128)} %bitcast.3) | data formatting | bytes 294912

commit v2 on v1

--- a/solution.py
+++ b/solution.py
@@ -145,7 +145,7 @@
 
 def kernel(sizes, block, links, solutions, force, *refs):
     (ul, utp, utm, uzp, uzm, urf, urb, urp, urm, uyp, uym, edges, far, xs,
-     xtp, xtm, xzp, xzm, xrf, xrb, ys, hy, hyn, ws, fs, gs, local, sends, recvs) = refs
+     hx, hxn, xrf, xrb, ys, hy, hyn, ws, fs, gs, local, sends, recvs) = refs
     blocks_t, blocks_z = block
     rows, lanes = ul.shape[-2:]
     solves = xs.shape[-2] // rows
@@ -160,6 +160,26 @@
             axis: m if c % n == 0 else lax.rem(m + (c % n), n)
             for axis, m, c, n in zip(AXES, me, step, sizes)
         }
+
+    def spinor(ref):
+        return ref[0], ref[1]
+
+    def gauge(ref, mu):
+        return ref[mu, 0], ref[mu, 1]
+
+    def put(ref, mu, value):
+        ref[mu, 0], ref[mu, 1] = value
+
+    def two(ref, mu):
+        return ref.at[mu, :, pl.ds(0, 2)]
+
+    def third(ref, mu):
+        re, im = gauge(ref, mu)
+        for c in range(3):
+            p, q = (c + 1) % 3, (c + 2) % 3
+            a, b, f, g = (0, p), (1, q), (0, q), (1, p)
+            ref[mu, 0, 2, c] = re[a] * re[b] - im[a] * im[b] - re[f] * re[g] + im[f] * im[g]
+            ref[mu, 1, 2, c] = re[f] * im[g] + im[f] * re[g] - re[a] * im[b] - im[a] * re[b]
 
     every_t, every_z = (0, blocks_t), (0, blocks_z)
 
@@ -219,6 +239,9 @@
         pl.semaphore_signal(barrier, inc=1, device_id=seat(step), device_id_type=MESH)
     for copy in locals_[:first_locals]:
         copy.wait()
+    x = spinor(xs)
+    for k, (mu, sign) in enumerate(((0, -1), (0, 1), (1, -1), (1, 1))):
+        put(hx, k, half(x, mu, sign))
     pl.semaphore_wait(barrier, len(peers))
 
     t_ahead, t_behind, z_ahead, z_behind = (1, 0, 0), (-1, 0, 0), (0, 1, 0), (0, -1, 0)
@@ -232,57 +255,48 @@
         spinor_boxes(source, (from_t, from_z), target, (to_t, to_z), lead,
                      lambda a, b: send(a, b, step))
 
-    sent_spinor(xs, zero, every_z, xtp, edge_t, every_z, 3, t_behind)
-    sent_spinor(xs, edge_t, every_z, xtm, zero, every_z, 3, t_ahead)
-    sent_spinor(xs, every_t, zero, xzp, every_t, edge_z, 3, z_behind)
-    sent_spinor(xs, every_t, edge_z, xzm, every_t, zero, 3, z_ahead)
-    sent(ul.at[0], edge_t, every_z, utm.at[0], zero, every_z, 3, t_ahead)
-    sent(ul.at[1], every_t, edge_z, uzm.at[1], every_t, zero, 3, z_ahead)
+    sent_spinor(hx.at[0], zero, every_z, hxn.at[0], edge_t, every_z, 3, t_behind)
+    sent_spinor(hx.at[1], edge_t, every_z, hxn.at[1], zero, every_z, 3, t_ahead)
+    sent_spinor(hx.at[2], every_t, zero, hxn.at[2], every_t, edge_z, 3, z_behind)
+    sent_spinor(hx.at[3], every_t, edge_z, hxn.at[3], every_t, zero, 3, z_ahead)
+    sent(two(ul, 0), edge_t, every_z, two(utm, 0), zero, every_z, 3, t_ahead)
+    sent(two(ul, 1), every_t, edge_z, two(uzm, 1), every_t, zero, 3, z_ahead)
     send(xs, xrf, r_prev)
     if not one_ring:
         send(xs, xrb, r_next)
     send(ul.at[2], urb.at[2], r_prev if one_ring else r_next)
     first_remotes = len(remotes)
     later, other = pl.ds(1, 3), pl.ds(2, 2)
-    sent(ul.at[later], zero, every_z, utp.at[later], edge_t, every_z, 4, t_behind)
-    sent(ul.at[later], edge_t, every_z, utm.at[later], zero, every_z, 4, t_ahead)
-    sent(ul.at[0], every_t, zero, uzp.at[0], every_t, edge_z, 3, z_behind)
-    sent(ul.at[other], every_t, zero, uzp.at[other], every_t, edge_z, 4, z_behind)
-    sent(ul.at[0], every_t, edge_z, uzm.at[0], every_t, zero, 3, z_ahead)
-    sent(ul.at[other], every_t, edge_z, uzm.at[other], every_t, zero, 4, z_ahead)
-    sent(ul.at[1], tail_t, edge_z, edges.at[0], head_t, zero, 3, z_ahead)
-    sent(ul.at[1], zero, edge_z, edges.at[0], edge_t, zero, 3, (-1, 1, 0))
-    sent(ul.at[1], zero, head_z, edges.at[0], edge_t, tail_z, 3, t_behind)
-    sent(ul.at[0], edge_t, tail_z, edges.at[1], zero, head_z, 3, t_ahead)
-    sent(ul.at[0], edge_t, zero, edges.at[1], zero, edge_z, 3, (1, -1, 0))
-    sent(ul.at[0], head_t, zero, edges.at[1], tail_t, edge_z, 3, z_behind)
-    sent(ul.at[2], zero, every_z, far.at[0], edge_t, every_z, 3, (-1, 0, 1))
-    sent(ul.at[0], edge_t, every_z, far.at[1], zero, every_z, 3, (1, 0, -1))
-    sent(ul.at[2], every_t, zero, far.at[2], every_t, edge_z, 3, (0, -1, 1))
-    sent(ul.at[1], every_t, edge_z, far.at[3], every_t, zero, 3, (0, 1, -1))
-    sent(ul.at[2], tail_t, every_z, far.at[0], head_t, every_z, 3, r_next)
-    sent(ul.at[0], head_t, every_z, far.at[1], tail_t, every_z, 3, r_prev)
-    sent(ul.at[2], every_t, tail_z, far.at[2], every_t, head_z, 3, r_next)
-    sent(ul.at[1], every_t, head_z, far.at[3], every_t, tail_z, 3, r_prev)
+    sent(two(ul, later), zero, every_z, two(utp, later), edge_t, every_z, 4, t_behind)
+    sent(two(ul, later), edge_t, every_z, two(utm, later), zero, every_z, 4, t_ahead)
+    sent(two(ul, 0), every_t, zero, two(uzp, 0), every_t, edge_z, 3, z_behind)
+    sent(two(ul, other), every_t, zero, two(uzp, other), every_t, edge_z, 4, z_behind)
+    sent(two(ul, 0), every_t, edge_z, two(uzm, 0), every_t, zero, 3, z_ahead)
+    sent(two(ul, other), every_t, edge_z, two(uzm, other), every_t, zero, 4, z_ahead)
+    sent(two(ul, 1), tail_t, edge_z, two(edges, 0), head_t, zero, 3, z_ahead)
+    sent(two(ul, 1), zero, edge_z, two(edges, 0), edge_t, zero, 3, (-1, 1, 0))
+    sent(two(ul, 1), zero, head_z, two(edges, 0), edge_t, tail_z, 3, t_behind)
+    sent(two(ul, 0), edge_t, tail_z, two(edges, 1), zero, head_z, 3, t_ahead)
+    sent(two(ul, 0), edge_t, zero, two(edges, 1), zero, edge_z, 3, (1, -1, 0))
+    sent(two(ul, 0), head_t, zero, two(edges, 1), tail_t, edge_z, 3, z_behind)
+    sent(two(ul, 2), zero, every_z, two(far, 0), edge_t, every_z, 3, (-1, 0, 1))
+    sent(two(ul, 0), edge_t, every_z, two(far, 1), zero, every_z, 3, (1, 0, -1))
+    sent(two(ul, 2), every_t, zero, two(far, 2), every_t, edge_z, 3, (0, -1, 1))
+    sent(two(ul, 1), every_t, edge_z, two(far, 3), every_t, zero, 3, (0, 1, -1))
+    sent(two(ul, 2), tail_t, every_z, two(far, 0), head_t, every_z, 3, r_next)
+    sent(two(ul, 0), head_t, every_z, two(far, 1), tail_t, every_z, 3, r_prev)
+    sent(two(ul, 2), every_t, tail_z, two(far, 2), every_t, head_z, 3, r_next)
+    sent(two(ul, 1), every_t, head_z, two(far, 3), every_t, tail_z, 3, r_prev)
     send(ul.at[pl.ds(0, 2)], urf.at[pl.ds(0, 2)], r_prev)
     send(ul.at[3], urf.at[3], r_prev)
     if not one_ring:
         send(ul.at[pl.ds(0, 2)], urb.at[pl.ds(0, 2)], r_next)
         send(ul.at[3], urb.at[3], r_next)
     link_remotes = len(remotes)
-    spinor_boxes(xs, (tail_t, every_z), xtp, (head_t, every_z), 3, bring)
-    spinor_boxes(xs, (head_t, every_z), xtm, (tail_t, every_z), 3, bring)
-    spinor_boxes(xs, (every_t, tail_z), xzp, (every_t, head_z), 3, bring)
-    spinor_boxes(xs, (every_t, head_z), xzm, (every_t, tail_z), 3, bring)
-
-    def spinor(ref):
-        return ref[0], ref[1]
-
-    def gauge(ref, mu):
-        return ref[mu, 0], ref[mu, 1]
-
-    def put(ref, mu, value):
-        ref[mu, 0], ref[mu, 1] = value
+    spinor_boxes(hx.at[0], (tail_t, every_z), hxn.at[0], (head_t, every_z), 3, bring)
+    spinor_boxes(hx.at[1], (head_t, every_z), hxn.at[1], (tail_t, every_z), 3, bring)
+    spinor_boxes(hx.at[2], (every_t, tail_z), hxn.at[2], (every_t, head_z), 3, bring)
+    spinor_boxes(hx.at[3], (every_t, head_z), hxn.at[3], (every_t, tail_z), 3, bring)
 
     def doubled(ref, mu):
         re, im = gauge(ref, mu)
@@ -318,6 +332,8 @@
     for copy in remotes[:first_remotes]:
         copy.wait_recv()
 
+    third(utm, 0)
+    third(uzm, 1)
     put(urm, 2, both(r_behind, gauge(ul, 2), gauge(urb, 2)))
 
     x = spinor(xs)
@@ -329,10 +345,10 @@
 
     for mu in range(4):
         if mu == 0:
-            ahead = signed(half(spinor(xtp), mu, -1), ahead_sign)
-            behind = signed(half(spinor(xtm), mu, 1), behind_sign)
+            ahead = signed(gauge(hxn, 0), ahead_sign)
+            behind = signed(gauge(hxn, 1), behind_sign)
         elif mu == 1:
-            ahead, behind = half(spinor(xzp), mu, -1), half(spinor(xzm), mu, 1)
+            ahead, behind = gauge(hxn, 2), gauge(hxn, 3)
         elif mu == 2:
             ahead = both(r_ahead, half(x, mu, -1), half(spinor(xrf), mu, -1))
             behind = both(r_behind, half(x, mu, 1), half(spinor(xrb), mu, 1))
@@ -360,6 +376,16 @@
     for copy in remotes[first_remotes:link_remotes]:
         copy.wait_recv()
 
+    for mu in (1, 2, 3):
+        third(utp, mu)
+        third(utm, mu)
+    for mu in (0, 2, 3):
+        third(uzp, mu)
+        third(uzm, mu)
+    for k in range(2):
+        third(edges, k)
+    for k in range(4):
+        third(far, k)
     for mu in (0, 1, 3):
         here = gauge(ul, mu)
         put(urp, mu, both(r_ahead, here, gauge(urf, mu)))
@@ -425,15 +451,15 @@
         for k, plane in enumerate(planes):
             if mu in plane:
                 parts = parts + fs[k, :, pl.ds(plane.index(mu) * rows, rows)]
-        third = (parts[6] + parts[7] + parts[8]) / 3.0
+        mean = (parts[6] + parts[7] + parts[8]) / 3.0
         for k, (i, j) in enumerate(((0, 1), (0, 2), (1, 2))):
             force[mu, 0, i, j] = parts[k]
             force[mu, 0, j, i] = -parts[k]
             force[mu, 1, i, j] = parts[3 + k]
             force[mu, 1, j, i] = parts[3 + k]
         for i in range(3):
-            force[mu, 0, i, i] = jnp.zeros_like(third)
-            force[mu, 1, i, i] = parts[6 + i] - third
+            force[mu, 0, i, i] = jnp.zeros_like(mean)
+            force[mu, 1, i, i] = parts[6 + i] - mean
 
     for copy in remotes:
         copy.wait_send()
@@ -456,13 +482,14 @@
     unused = vmem(8, lanes) if sizes[2] == 2 else None
     small = links.shape[1:]
     h = vmem(3, c, 2, a, n * rows, lanes)
+    h4 = vmem(4, c, 2, a, n * rows, lanes)
     out = pl.pallas_call(
         functools.partial(kernel, sizes, block),
         out_shape=jax.ShapeDtypeStruct(links.shape, jnp.float32),
         in_specs=[pl.BlockSpec(memory_space=pl.ANY)] * 2,
         out_specs=pl.BlockSpec(memory_space=pltpu.VMEM),
         scratch_shapes=[u] * 6 + [unused or u] + [u] * 4 + [vmem(12, *small), vmem(4, *small)]
-        + [x] * 6 + [unused or x] + [x, h, h]
+        + [x, h4, h4, x, unused or x, x, h, h]
         + [vmem(4, c, 2, a, n * rows, lanes), vmem(6, 9, 2 * rows, lanes),
            vmem(4, 9, n * rows, lanes)]
         + [pltpu.SemaphoreType.DMA((LOCAL_COPIES,)), pltpu.SemaphoreType.DMA((REMOTE_COPIES,)),

time: 21.1 us -> 18.9 us (0.90)
  Pallas kernels: 19.3 us -> 17.2 us
    pallas_call x1, Pallas kernels: 19.3 us -> 17.2 us  [on_device(): pl.pallas_call(functools.partial(kernel, sizes, block), out_shape=jax.Sha...]
where the time goes in v2:
time: 18.9 us; the launch traced here: 18.8 us
  Pallas kernels  17.2 us (91%)
  local copies, waits for them, and re-layouts  1.59 us (8%)
    pallas_call x1, Pallas kernels, on_device(): pl.pallas_call(functools.partial(kernel, sizes, block), out_shape=jax.Sha...  17.2 us
    unnamed x1, local copies, waits for them, and re-layouts  1.59 us

profile of v2, /device:TPU:0, one launch (start us, length us, event | category | flops | bytes accessed | tf_op | source)
XLA Modules:
  0.0 18.8 jit_solution(8813929736471439701)
XLA Ops:
  0.0 17.2 %shard_map.28 = f32[4,2,3,3,4,128]{5,4,3,2,1,0:T(4,128)} custom-call(f32[4,2,3,3,4,128]{5,4,3,2,1,0:T(4,128)} %bitcast.4, f32[2,2,4,3,4,128]{5,4,3,2,1,0:T(4,128)} %bitcast.5), custom_call_target="tpu_custom_call" | custom-call | tf_op jit(solution)/shard_map/pallas_call | solution.py:486
  17.2 1.6 %copy.4 = f32[4,2,3,3,2,2,128]{6,5,4,3,2,1,0:T(2,128)} copy(f32[4,2,3,3,2,2,128]{6,5,4,3,2,1,0:T(2,128)} %bitcast.3) | data formatting | bytes 294912

commit v3 on v2

--- a/solution.py
+++ b/solution.py
@@ -180,6 +180,12 @@
             a, b, f, g = (0, p), (1, q), (0, q), (1, p)
             ref[mu, 0, 2, c] = re[a] * re[b] - im[a] * im[b] - re[f] * re[g] + im[f] * im[g]
             ref[mu, 1, 2, c] = re[f] * im[g] + im[f] * re[g] - re[a] * im[b] - im[a] * re[b]
+
+    def moved_rows(ref, mu, from_box, slot, to_box):
+        for (a, n), (b, _) in zip(runs(*from_box), runs(*to_box)):
+            for part in range(2):
+                block = ref[mu, part, pl.ds(0, 2), :, pl.ds(a, n)]
+                edges[slot, part, pl.ds(0, 2), :, pl.ds(b, n)] = block
 
     every_t, every_z = (0, blocks_t), (0, blocks_z)
 
@@ -273,12 +279,8 @@
     sent(two(ul, other), every_t, zero, two(uzp, other), every_t, edge_z, 4, z_behind)
     sent(two(ul, 0), every_t, edge_z, two(uzm, 0), every_t, zero, 3, z_ahead)
     sent(two(ul, other), every_t, edge_z, two(uzm, other), every_t, zero, 4, z_ahead)
-    sent(two(ul, 1), tail_t, edge_z, two(edges, 0), head_t, zero, 3, z_ahead)
     sent(two(ul, 1), zero, edge_z, two(edges, 0), edge_t, zero, 3, (-1, 1, 0))
-    sent(two(ul, 1), zero, head_z, two(edges, 0), edge_t, tail_z, 3, t_behind)
-    sent(two(ul, 0), edge_t, tail_z, two(edges, 1), zero, head_z, 3, t_ahead)
     sent(two(ul, 0), edge_t, zero, two(edges, 1), zero, edge_z, 3, (1, -1, 0))
-    sent(two(ul, 0), head_t, zero, two(edges, 1), tail_t, edge_z, 3, z_behind)
     sent(two(ul, 2), zero, every_z, two(far, 0), edge_t, every_z, 3, (-1, 0, 1))
     sent(two(ul, 0), edge_t, every_z, two(far, 1), zero, every_z, 3, (1, 0, -1))
     sent(two(ul, 2), every_t, zero, two(far, 2), every_t, edge_z, 3, (0, -1, 1))
@@ -382,6 +384,10 @@
     for mu in (0, 2, 3):
         third(uzp, mu)
         third(uzm, mu)
+    moved_rows(utp, 1, (edge_t, head_z), 0, (edge_t, tail_z))
+    moved_rows(uzm, 1, (tail_t, zero), 0, (head_t, zero))
+    moved_rows(utm, 0, (zero, tail_z), 1, (zero, head_z))
+    moved_rows(uzp, 0, (head_t, edge_z), 1, (tail_t, edge_z))
     for k in range(2):
         third(edges, k)
     for k in range(4):
@@ -451,15 +457,7 @@
         for k, plane in enumerate(planes):
             if mu in plane:
                 parts = parts + fs[k, :, pl.ds(plane.index(mu) * rows, rows)]
-        mean = (parts[6] + parts[7] + parts[8]) / 3.0
-        for k, (i, j) in enumerate(((0, 1), (0, 2), (1, 2))):
-            force[mu, 0, i, j] = parts[k]
-            force[mu, 0, j, i] = -parts[k]
-            force[mu, 1, i, j] = parts[3 + k]
-            force[mu, 1, j, i] = parts[3 + k]
-        for i in range(3):
-            force[mu, 0, i, i] = jnp.zeros_like(mean)
-            force[mu, 1, i, i] = parts[6 + i] - mean
+        force[mu] = parts
 
     for copy in remotes:
         copy.wait_send()
@@ -485,7 +483,7 @@
     h4 = vmem(4, c, 2, a, n * rows, lanes)
     out = pl.pallas_call(
         functools.partial(kernel, sizes, block),
-        out_shape=jax.ShapeDtypeStruct(links.shape, jnp.float32),
+        out_shape=jax.ShapeDtypeStruct((whole[0], 9, rows, lanes), jnp.float32),
         in_specs=[pl.BlockSpec(memory_space=pl.ANY)] * 2,
         out_specs=pl.BlockSpec(memory_space=pltpu.VMEM),
         scratch_shapes=[u] * 6 + [unused or u] + [u] * 4 + [vmem(12, *small), vmem(4, *small)]
@@ -496,7 +494,28 @@
            pltpu.SemaphoreType.DMA((REMOTE_COPIES,))],
         compiler_params=pltpu.CompilerParams(collective_id=0, has_side_effects=True),
     )(links, solutions)
+    out = pl.pallas_call(
+        assembled,
+        out_shape=jax.ShapeDtypeStruct(links.shape, jnp.float32),
+        in_specs=[pl.BlockSpec(memory_space=pltpu.VMEM)],
+        out_specs=pl.BlockSpec(memory_space=pltpu.VMEM),
+        compiler_params=pltpu.CompilerParams(vmem_limit_bytes=8 * 2**20),
+    )(out)
     return out.reshape(whole)
+
+
+def assembled(nines, force):
+    for mu in range(nines.shape[0]):
+        parts = nines[mu]
+        mean = (parts[6] + parts[7] + parts[8]) / 3.0
+        for k, (i, j) in enumerate(((0, 1), (0, 2), (1, 2))):
+            force[mu, 0, i, j] = parts[k]
+            force[mu, 0, j, i] = -parts[k]
+            force[mu, 1, i, j] = parts[3 + k]
+            force[mu, 1, j, i] = parts[3 + k]
+        for i in range(3):
+            force[mu, 0, i, i] = jnp.zeros_like(mean)
+            force[mu, 1, i, i] = parts[6 + i] - mean
 
 
 def solution(mesh):

time: 18.9 us -> 18.6 us (0.984)
  local copies, waits for them, and re-layouts: 1.59 us -> 0.88 us
  Pallas kernels: 17.2 us -> 17.6 us
    unnamed x1 -> x2, local copies, waits for them, and re-layouts: 1.59 us -> 0.88 us
    pallas_call x0 -> x1, Pallas kernels: none -> 0.68 us  [on_device(): pl.pallas_call(assembled, out_shape=jax.ShapeDtypeStruct(links.shape, jnp...]
    pallas_call x1, Pallas kernels: 17.2 us -> 16.9 us  [on_device(): pl.pallas_call(functools.partial(kernel, sizes, block), out_shape=jax.Sha...]
where the time goes in v3:
time: 18.6 us; the launch traced here: 18.4 us
  Pallas kernels  17.6 us (95%)
  local copies, waits for them, and re-layouts  0.88 us (5%)
    pallas_call x1, Pallas kernels, on_device(): pl.pallas_call(functools.partial(kernel, sizes, block), out_shape=jax.Sha...  16.9 us
    unnamed x2, local copies, waits for them, and re-layouts  0.88 us
    pallas_call x1, Pallas kernels, on_device(): pl.pallas_call(assembled, out_shape=jax.ShapeDtypeStruct(links.shape, jnp...  0.68 us

profile of v3, /device:TPU:0, one launch (start us, length us, event | category | flops | bytes accessed | tf_op | source)
XLA Modules:
  0.0 18.4 jit_solution(7910939198422011804)
XLA Ops:
  0.0 16.9 %shard_map.28.nines = f32[4,9,4,128]{3,2,1,0:T(4,128)} custom-call(f32[4,2,3,3,4,128]{5,4,3,2,1,0:T(4,128)} %bitcast.3, f32[2,2,4,3,4,128]{5,4,3,2,1,0:T(4,128)} %bitcast.4), custom_call_target="tpu_custom_call" | custom-call | tf_op jit(solution)/shard_map/pallas_call | solution.py:484
  16.9 0.0 copy-start
  16.9 0.9 %copy-done = f32[4,9,4,128]{3,2,1,0:T(4,128)S(1)} copy-done((f32[4,9,4,128]{3,2,1,0:T(4,128)S(1)}, f32[4,9,4,128]{3,2,1,0:T(4,128)}, u32[]{:S(2)}) %copy-start) | copy-done | bytes 73752
  17.8 0.7 %shard_map.29 = f32[4,2,3,3,4,128]{5,4,3,2,1,0:T(4,128)} custom-call(f32[4,9,4,128]{3,2,1,0:T(4,128)S(1)} %copy-done), custom_call_target="tpu_custom_call" | custom-call | tf_op jit(solution)/shard_map/pallas_call | solution.py:497
Async XLA Ops:
  16.9 0.9 %copy-start = (f32[4,9,4,128]{3,2,1,0:T(4,128)S(1)}, f32[4,9,4,128]{3,2,1,0:T(4,128)}, u32[]{:S(2)}) copy-start(f32[4,9,4,128]{3,2,1,0:T(4,128)} %shard_map.28.nines) | copy-start | bytes 221188
